TPU v7x, 32 devices: a whole 2x2x4 slice. The times are simulated.
32 devices in a mesh: sub: 8 (over z, y), leaf: 4 (over x, core).
Axes of the slice: x: 2, y: 2, z: 4, core: 2. Of those that a mesh axis runs over, the one named last changes fastest.
Arguments:
- child_row: int32 [16], P('sub'), may hold values from 0 to 15, each once
- counts: int32 [16], P('sub'), may hold values from 1 to 16, as said below
- live_mask: int32 [16, 16, 1326], P('sub', 'leaf'), may hold values 0 or 1
- hand_rank: int32 [16, 16, 1326], P('sub', 'leaf'), may hold values from 0 to 7461
- bet_size: float32 [16, 8], P('sub'), may hold values from 0.25 to 4
- pot_size: float32 [16], P('sub'), may hold values from 4 to 16
- trunk_ranges: float32 [16, 2, 1326], P('sub'), may hold values from 0.05 to 1
- trunk_values: float32 [16, 1326], P('sub'), may hold values from -8 to 8
Outputs:
- root_values: float32 [16, 2, 1326], P('sub')
Inputs may be any that keep to these rules, and one draw needn't show every extreme that they name: Subgame s reads and returns row child_row[s] of the trunk's arrays; every row is named by exactly one subgame. Leaf blocks b < counts[s] of subgame s are used; some subgame uses all 16.
All inputs are finite; a program needn't handle non-finite values. No bound on the sum of `live_mask` on one device may be relied on, other than what follows from the above.
Results may differ from a plain program's by a relative error of at most 0.0004.
Values sent between devices are 32-bit elements; how exact they have to be, the bound alone decides.
A program may use at most 64 MiB of HBM per device.

v0:
```python
import jax
import jax.numpy as jnp
from jax import lax
from jax.sharding import PartitionSpec as P

ACT = 8
ITERS = 4


smooth = 0.1


def regret_match(positive, total_sum, option_count):
    return (positive + smooth) / (total_sum + option_count * smooth)


def leaf_piece(source, leaves, leaf_index):
    hands_total = source.shape[-1]
    share_len = -(-hands_total // leaves)
    padding = [(0, 0)] * (source.ndim - 1) + [(0, share_len * leaves - hands_total)]
    padded = jnp.pad(source, padding)
    return lax.dynamic_slice_in_dim(padded, leaf_index * share_len, share_len, source.ndim - 1)


def apply_blocks(rank_rows, live_rows, column_sets):
    hands_total = rank_rows.shape[-1]
    half_rows = hands_total // 2

    def one_block(scan_state, inputs):
        rank_row, live_row, column_set = inputs
        tile_list = []
        for offset in (0, half_rows):
            rows_rank = rank_row[offset : offset + half_rows]
            rows_live = live_row[offset : offset + half_rows]
            sign_tile = jnp.sign(rows_rank[:, None] - rank_row[None, :]).astype(jnp.bfloat16)
            matrix = sign_tile * rows_live[:, None] * live_row[None, :]
            tile_list.append(
                lax.dot_general(
                    column_set, matrix, (((1,), (1,)), ((), ())), preferred_element_type=jnp.float32
                )
            )
        return (scan_state, jnp.concatenate(tile_list, axis=1))

    unused, result = lax.scan(
        one_block, jnp.zeros((), jnp.int32), (rank_rows, live_rows, column_sets)
    )
    return result


def shards(child_row, counts, live_mask, hand_rank, bet_size, pot_size, trunk_ranges, trunk_values):
    leaves = lax.axis_size("leaf")
    leaf_index = lax.axis_index("leaf")
    hands_total = trunk_ranges.shape[-1]
    all_ranges, all_values = (
        lax.all_gather(trunk_ranges, "sub", axis=0, tiled=True),
        lax.all_gather(trunk_values, "sub", axis=0, tiled=True),
    )
    ranges = jnp.take(all_ranges, child_row, axis=0)
    values = jnp.take(all_values, child_row, axis=0)
    own_range = ranges[:, 0]
    opp_range = ranges[:, 1]
    local_subs = live_mask.shape[0]
    block_count = live_mask.shape[1]
    live_real = live_mask.astype(jnp.float32)
    live_half = live_mask.astype(jnp.bfloat16).reshape(local_subs * block_count, hands_total)
    rank_rows = hand_rank.reshape(local_subs * block_count, hands_total)
    global_block = leaf_index * block_count + jnp.arange(block_count)
    block_weight = jnp.where(global_block[None, :] < counts[:, None], 1.0, 0.0) / counts[
        :, None
    ].astype(jnp.float32)
    weight = block_weight[:, :, None, None]
    factor = pot_size[:, None] * (1.0 + bet_size) / hands_total
    regret_own = jnp.zeros((local_subs, ACT, hands_total), jnp.float32)
    call_regret = jnp.zeros((local_subs, block_count, ACT, hands_total), jnp.float32)
    fold_regret = jnp.zeros((local_subs, block_count, ACT, hands_total), jnp.float32)
    follow_regret = jnp.zeros((local_subs, hands_total), jnp.float32)
    stop_regret = jnp.zeros((local_subs, hands_total), jnp.float32)
    for step_index in range(ITERS):
        own_strategy = regret_match(regret_own, jnp.sum(regret_own, axis=1, keepdims=True), ACT)
        call_prob = regret_match(call_regret, call_regret + fold_regret, 2)
        follow = regret_match(follow_regret, follow_regret + stop_regret, 2)
        reach_own = (own_range[:, None, :] * own_strategy).astype(jnp.bfloat16)
        entering = opp_range * follow
        reach_call = (entering[:, None, None, :] * call_prob).astype(jnp.bfloat16)
        reach_fold = entering[:, None, None, :] * (1.0 - call_prob)
        column_sets = jnp.concatenate(
            [reach_call, jnp.broadcast_to(reach_own[:, None], reach_call.shape)], axis=2
        )
        column_sets = column_sets.reshape(local_subs * block_count, 2 * ACT, hands_total)
        applied = apply_blocks(rank_rows, live_half, column_sets).reshape(
            local_subs, block_count, 2 * ACT, hands_total
        )
        showdown_own = applied[:, :, :ACT]
        showdown_opp = applied[:, :, ACT:]
        own_real = reach_own.astype(jnp.float32)
        fold_mass = jnp.sum(live_real[:, :, None, :] * reach_fold, axis=-1) / hands_total
        own_mass = jnp.sum(live_real[:, :, None, :] * own_real[:, None], axis=-1) / hands_total
        per_block = (
            factor[:, None, :, None] * showdown_own
            + live_real[:, :, None, :] * (pot_size[:, None, None] * fold_mass)[..., None]
        )
        partial_own = jnp.sum(weight * per_block, axis=1)
        call_value = factor[:, None, :, None] * showdown_opp
        fold_value = -live_real[:, :, None, :] * (pot_size[:, None, None] * own_mass)[..., None]
        node_value = call_prob * call_value + (1.0 - call_prob) * fold_value
        partial_follow = jnp.sum(weight * node_value, axis=(1, 2))
        value_own, follow_value = lax.psum((partial_own, partial_follow), "leaf")
        gadget_value = follow * follow_value + (1.0 - follow) * values
        root_value = jnp.sum(own_strategy * value_own, axis=1)
        if step_index + 1 < ITERS:
            regret_own = jnp.maximum(regret_own + value_own - root_value[:, None, :], 0.0)
            call_regret = jnp.maximum(call_regret + call_value - node_value, 0.0)
            fold_regret = jnp.maximum(fold_regret + fold_value - node_value, 0.0)
            follow_regret = jnp.maximum(follow_regret + follow_value - gadget_value, 0.0)
            stop_regret = jnp.maximum(stop_regret + values - gadget_value, 0.0)
    results = jnp.stack([root_value, jnp.maximum(values, follow_value)], axis=1)
    total_rows = lax.axis_size("sub") * local_subs
    hand_part = leaf_piece(results, leaves, leaf_index)
    dense_rows = (
        jnp.zeros((total_rows, 2, hand_part.shape[-1]), jnp.float32).at[child_row].set(hand_part)
    )
    summed = lax.psum_scatter(dense_rows, "sub", scatter_dimension=0, tiled=True)
    joined = lax.all_gather(summed, "leaf", axis=2, tiled=True)
    answer = joined[..., :hands_total]
    return answer


def solution(mesh):
    in_specs = (
        P("sub"),
        P("sub"),
        P("sub", "leaf", None),
        P("sub", "leaf", None),
        P("sub", None),
        P("sub"),
        P("sub", None, None),
        P("sub", None),
    )
    out_specs = P("sub", None, None)
    return jax.shard_map(shards, mesh=mesh, in_specs=in_specs, out_specs=out_specs, check_vma=False)
```

profile of v0, /device:TPU:0, one launch (start us, length us, event | category | flops | bytes accessed | tf_op | source)
XLA Modules:
  0.0 372.5 jit_solution(9653676023410397495)
XLA Ops:
  7.9 32.6 %all_gather.9 = f32[16,2,1326]{2,1,0:T(2,128)S(1)} all-gather(f32[2,2,1326]{2,1,0:T(2,128)} %param.22), channel_id=1, replica_groups=mesh['sub'=8,'leaf'=4] {'sub'}, dimensions={0}, use_global_device_ids=true | all-gather | bytes 190944 | tf_op jit(solution)/shard_map/all_gather | solution.py:55
  43.8 22.7 %while.40 = (s32[]{:T(128)}, f32[8,16,1326]{2,1,0:T(8,128)S(1)}, bf16[8,16,1326]{2,1,0:T(8,128)(2,1)S(1)}, s32[8,1326]{1,0:T(8,128)S(1)}, bf16[8,1326]{1,0:T(8,128)(2,1)S(1)}, /*index=5*/s32[]{:T(128)}, s32[]{:T(128)}, s32[]{}) while((s32[]{:T(128)}, f32[8,16,1326]{2,1,0:T(8,128)S(1)}, bf16[8,16,1326]{2,1,0:T(8,128)(2,1)S(1)}, ...), condition=%wide.region_1.2_spmd, body=%wide.region_0.1_spmd.sunk | while | flops 65077432 | bytes 432213 | solution.py:44
  45.3 1.2 fusion.167
  46.9 1.2 fusion.168
  48.1 1.2 fusion.167
  49.8 1.2 fusion.168
  50.9 1.2 fusion.167
  53.8 1.2 fusion.167
  56.6 1.2 fusion.167
  58.3 1.2 fusion.168
  59.5 1.2 fusion.167
  61.1 1.2 fusion.168
  62.3 1.3 fusion.167
  65.1 1.2 fusion.167
  67.9 10.3 %psum.57 = f32[2,1326]{1,0:T(2,128)S(1)} all-reduce(f32[2,1326]{1,0:T(2,128)S(1)} %get-tuple-element.137), channel_id=1, replica_groups=mesh['sub'=8,'leaf'=4] {'leaf'}, use_global_device_ids=true, to_apply=%region_8.9 | all-reduce | flops 2652 | bytes 21216 | tf_op jit(solution)/shard_map/psum | solution.py:107
  78.2 30.5 %all-gather = f32[8,2,1326]{2,1,0:T(2,128)S(1)} all-gather(f32[1,2,1326]{2,1,0:T(2,128)S(1)} %bitcast.114), channel_id=1, replica_groups=mesh['sub'=8,'leaf'=4] {'sub'}, dimensions={0}, use_global_device_ids=true | all-gather | bytes 95472 | tf_op jit(solution)/shard_map/all_gather | solution.py:56
  111.2 22.7 %while.41 = (s32[]{:T(128)}, f32[8,16,1326]{2,1,0:T(8,128)S(1)}, bf16[8,16,1326]{2,1,0:T(8,128)(2,1)S(1)}, s32[8,1326]{1,0:T(8,128)S(1)}, bf16[8,1326]{1,0:T(8,128)(2,1)S(1)}, /*index=5*/s32[]{:T(128)}, s32[]{:T(128)}, s32[]{}) while((s32[]{:T(128)}, f32[8,16,1326]{2,1,0:T(8,128)S(1)}, bf16[8,16,1326]{2,1,0:T(8,128)(2,1)S(1)}, ...), condition=%wide.region_11.12_spmd, body=%wide.region_10.11_spmd.sunk | while | flops 65077432 | bytes 432213 | solution.py:44
  112.7 1.2 fusion.174
  115.5 1.2 fusion.174
  118.3 1.2 fusion.174
  120.0 1.2 fusion.175
  121.2 1.2 fusion.174
  124.0 1.2 fusion.174
  125.6 1.2 fusion.175
  126.8 1.3 fusion.174
  128.5 1.2 fusion.175
  129.7 1.2 fusion.174
  131.3 1.2 fusion.175
  132.5 1.2 fusion.174
  136.0 31.0 %all-reduce.9.cloned.1.call-done = f32[2,8,1326]{2,1,0:T(8,128)} async-done(((f32[2,8,1326]{2,1,0:T(8,128)}), f32[2,8,1326]{2,1,0:T(8,128)}) %all-reduce.9.cloned.1.call-update) | async-done | bytes 84880 | tf_op jit(solution)/shard_map/psum | solution.py:107
  169.0 10.1 %psum.59 = f32[2,1326]{1,0:T(2,128)S(1)} all-reduce(f32[2,1326]{1,0:T(2,128)S(1)} %get-tuple-element.194), channel_id=1, replica_groups=mesh['sub'=8,'leaf'=4] {'leaf'}, use_global_device_ids=true, to_apply=%region_18.19 | all-reduce | flops 2652 | bytes 21216 | tf_op jit(solution)/shard_map/psum | solution.py:107
  179.9 22.7 %while.42 = (s32[]{:T(128)}, f32[8,16,1326]{2,1,0:T(8,128)S(1)}, bf16[8,16,1326]{2,1,0:T(8,128)(2,1)S(1)}, s32[8,1326]{1,0:T(8,128)S(1)}, bf16[8,1326]{1,0:T(8,128)(2,1)S(1)}, /*index=5*/s32[]{:T(128)}, s32[]{:T(128)}, s32[]{}) while((s32[]{:T(128)}, f32[8,16,1326]{2,1,0:T(8,128)S(1)}, bf16[8,16,1326]{2,1,0:T(8,128)(2,1)S(1)}, ...), condition=%wide.region_21.22_spmd, body=%wide.region_20.21_spmd.sunk | while | flops 65077432 | bytes 432213 | solution.py:44
  181.4 1.2 fusion.181
  184.2 1.2 fusion.181
  185.8 1.2 fusion.182
  187.0 1.2 fusion.181
  188.7 1.2 fusion.182
  189.9 1.2 fusion.181
  192.7 1.2 fusion.181
  195.5 1.2 fusion.181
  197.2 1.2 fusion.182
  198.4 1.2 fusion.181
  200.0 1.2 fusion.182
  201.2 1.2 fusion.181
  203.6 10.1 %psum.61 = f32[2,1326]{1,0:T(2,128)S(1)} all-reduce(f32[2,1326]{1,0:T(2,128)S(1)} %get-tuple-element.135), channel_id=1, replica_groups=mesh['sub'=8,'leaf'=4] {'leaf'}, use_global_device_ids=true, to_apply=%region_29.30 | all-reduce | flops 2652 | bytes 21216 | tf_op jit(solution)/shard_map/psum | solution.py:107
  214.0 31.5 %all-reduce.11.cloned.1.call-done = f32[2,8,1326]{2,1,0:T(8,128)} async-done(((f32[2,8,1326]{2,1,0:T(8,128)}), f32[2,8,1326]{2,1,0:T(8,128)}) %all-reduce.11.cloned.1.call-update) | async-done | bytes 84880 | tf_op jit(solution)/shard_map/psum | solution.py:107
  247.3 22.7 %while.43 = (s32[]{:T(128)}, f32[8,16,1326]{2,1,0:T(8,128)S(1)}, bf16[8,16,1326]{2,1,0:T(8,128)(2,1)S(1)}, s32[8,1326]{1,0:T(8,128)S(1)}, bf16[8,1326]{1,0:T(8,128)(2,1)S(1)}, /*index=5*/s32[]{:T(128)}, s32[]{:T(128)}, s32[]{}) while((s32[]{:T(128)}, f32[8,16,1326]{2,1,0:T(8,128)S(1)}, bf16[8,16,1326]{2,1,0:T(8,128)(2,1)S(1)}, ...), condition=%wide.region_31.32_spmd, body=%wide.region_30.31_spmd.sunk | while | flops 65077432 | bytes 432213 | solution.py:44
  247.6 1.2 fusion.189
  248.8 1.2 fusion.188
  250.4 1.2 fusion.189
  251.6 1.2 fusion.188
  254.5 1.2 fusion.188
  257.3 1.2 fusion.188
  259.0 1.2 fusion.189
  260.2 1.2 fusion.188
  261.8 1.2 fusion.189
  263.0 1.2 fusion.188
  265.8 1.2 fusion.188
  268.7 1.2 fusion.188
  271.1 10.1 %psum.63 = f32[2,1326]{1,0:T(2,128)S(1)} all-reduce(f32[2,1326]{1,0:T(2,128)S(1)} %get-tuple-element.133), channel_id=1, replica_groups=mesh['sub'=8,'leaf'=4] {'leaf'}, use_global_device_ids=true, to_apply=%region_38.39 | all-reduce | flops 2652 | bytes 21216 | tf_op jit(solution)/shard_map/psum | solution.py:107
  281.3 31.7 %all-reduce.13.cloned.1.call-done = f32[2,8,1326]{2,1,0:T(8,128)} async-done(((f32[2,8,1326]{2,1,0:T(8,128)}), f32[2,8,1326]{2,1,0:T(8,128)}) %all-reduce.13.cloned.1.call-update) | async-done | bytes 84880 | tf_op jit(solution)/shard_map/psum | solution.py:107
  314.6 37.5 %all-reduce.1 = f32[16,2,332]{2,1,0:T(2,128)S(1)} all-reduce(f32[16,2,332]{2,1,0:T(2,128)S(1)} %scatter_fusion), channel_id=2, replica_groups=mesh['sub'=8,'leaf'=4] {'sub'}, use_global_device_ids=true, to_apply=%region_40.41.clone | all-reduce | flops 10624 | bytes 84992
  352.4 11.4 %all_gather.11 = f32[2,2,1328]{1,0,2:T(2,128)S(1)} all-gather(f32[2,2,332]{1,0,2:T(2,128)S(1)} %copy.11), channel_id=1, replica_groups=mesh['sub'=8,'leaf'=4] {'leaf'}, dimensions={2}, use_global_device_ids=true | all-gather | bytes 26560 | tf_op jit(solution)/shard_map/all_gather | solution.py:123
  364.0 2.1 copy.12
  (273 shorter events, 50.0 us)
Async XLA Ops:
  6.5 103.4 %all-reduce.7.cloned.1.call-start = ((), (), s32[]{:S(2)}) async-start(), calls=%async_computation | async-start | bytes 180224 | tf_op jit(solution)/shard_map/psum | solution.py:107
  43.7 22.8 %copy-start.4 = (f32[2,8]{1,0:T(2,128)S(1)}, f32[2,8]{1,0:T(2,128)}, u32[]{:S(2)}) copy-start(f32[2,8]{1,0:T(2,128)} %param.20) | copy-start | bytes 196
  43.7 22.8 %copy-start.5 = (f32[2]{0:T(128)S(1)}, f32[2]{0:T(128)}, u32[]{:S(2)}) copy-start(f32[2]{0:T(128)} %param.21) | copy-start | bytes 28
  43.8 22.8 %copy-start = (s32[2,4,1326]{2,1,0:T(4,128)S(1)}, s32[2,4,1326]{2,1,0:T(4,128)}, u32[]{:S(2)}) copy-start(s32[2,4,1326]{2,1,0:T(4,128)} %param.18) | copy-start | bytes 127300
  43.8 22.9 %copy-start.6 = (s32[2]{0:T(128)S(1)}, s32[2]{0:T(128)}, u32[]{:S(2)}) copy-start(s32[2]{0:T(128)} %param.17) | copy-start | bytes 28
  43.8 34.4 %copy-start.3 = (f32[2,1326]{1,0:T(2,128)S(1)}, f32[2,1326]{1,0:T(2,128)}, u32[]{:S(2)}) copy-start(f32[2,1326]{1,0:T(2,128)} %param.23) | copy-start | bytes 31828
  67.8 99.2 %all-reduce.9.cloned.1.call-start = ((), (), s32[]{:S(2)}) async-start(), calls=%async_computation.1 | async-start | bytes 180224 | tf_op jit(solution)/shard_map/psum | solution.py:107
  111.2 23.6 %copy-start.7 = (u32[32]{0:T(128)S(1)}, u32[32]{0:T(128)}, u32[]{:S(2)}) copy-start(u32[32]{0:T(128)} %constant.137) | copy-start | bytes 388
  134.7 110.8 %all-reduce.11.cloned.1.call-start = ((), (), s32[]{:S(2)}) async-start(), calls=%async_computation.2 | async-start | bytes 180224 | tf_op jit(solution)/shard_map/psum | solution.py:107
  168.1 0.6 copy-start.1
  202.6 42.9 %copy-start.2 = (f32[2,8,1326]{2,1,0:T(8,128)S(1)}, f32[2,8,1326]{2,1,0:T(8,128)}, u32[]{:S(2)}) copy-start(f32[2,8,1326]{2,1,0:T(8,128)} %copy-done.1) | copy-start | bytes 254596
  213.7 99.2 %all-reduce.13.cloned.1.call-start = ((), (), s32[]{:S(2)}) async-start(), calls=%async_computation.3 | async-start | bytes 180224 | tf_op jit(solution)/shard_map/psum | solution.py:107
Sparse Core Ops, SparseCore 0:
  67.9 31.8 all-reduce.6
  134.8 32.1 all-reduce.8
  213.8 31.6 all-reduce.10
  281.3 31.5 all-reduce.12
where the time goes:
time: 373 us
  blocking collectives  153 us (41%)
  waiting for transfers between devices  94.3 us (25%)
  matrix products  77.9 us (21%)
  other arithmetic  17.5 us (5%)
  local copies, waits for them, and re-layouts  15.1 us (4%)
  between operations  14.2 us (4%)
    psum x4, waiting for transfers between devices, shards(): value_own, follow_value = lax.psum((partial_own, partial_follow), 'leaf')  94.2 us
    dot_general x64, matrix products, one_block(): lax.dot_general(column_set, matrix, (((1,), (1,)), ((), ())), preferred_e...  77.9 us
    psum x4, blocking collectives, shards(): value_own, follow_value = lax.psum((partial_own, partial_follow), 'leaf')  40.6 us
    unnamed x1, blocking collectives  37.5 us
    all_gather x1, blocking collectives, shards(): lax.all_gather(trunk_ranges, 'sub', axis=0, tiled=True)  32.6 us
    all_gather x1, blocking collectives, shards(): lax.all_gather(trunk_values, 'sub', axis=0, tiled=True)  30.5 us
    all_gather x1, blocking collectives, shards(): joined = lax.all_gather(summed, 'leaf', axis=2, tiled=True)  11.4 us
  transfers between devices with their start and end apart: 4, of which 3 were waited for; matrix products, arithmetic and copies ran while one was open for 1% of the time, Pallas kernels for 0%

commit v1 on v0

v1 whole, which is shorter than its diff:
```python
import functools

import jax
import jax.numpy as jnp
from jax import lax
from jax.experimental import pallas as pl
from jax.experimental.pallas import tpu as pltpu
from jax.sharding import PartitionSpec as P

ACT = 8
ITERS = 4
smooth = 0.1
LANES = 128
ROWS = 32


def solve_kernel(
    subs, leaves, hands, wide, local, blocks,
    row_ref, count_ref, bet_ref, pot_ref, live_ref, rank_ref, range_ref, value_ref,
    out_ref,
    matrix, rank_pad, live, call_regret, fold_regret, regret_own, follow_regret, stop_regret,
    own_range, opp_range, values, strategy, follow, reach,
    sum_own, sum_follow, all_range, all_value, all_row, final,
    range_send, range_recv, value_send, value_recv, row_send, row_recv,
    own_send, own_recv, follow_send, follow_recv, final_send, final_recv,
):
    me = lax.axis_index("sub")
    leaf = lax.axis_index("leaf")
    f32 = jnp.float32

    barrier = pltpu.get_barrier_semaphore()

    def sub_peer(k):
        return lax.rem(me + k, subs)

    def greet(k, carry):
        pl.semaphore_signal(barrier, inc=1, device_id={"sub": sub_peer(k)}, device_id_type=pl.DeviceIdType.MESH)
        return carry

    lax.fori_loop(1, subs, greet, 0)
    leaf_peers = [lax.rem(leaf + k, leaves) for k in range(1, leaves)]
    for peer in leaf_peers:
        pl.semaphore_signal(barrier, inc=1, device_id={"leaf": peer}, device_id_type=pl.DeviceIdType.MESH)

    rank_pad[...] = jnp.zeros_like(rank_pad)
    live[...] = jnp.zeros_like(live)
    for s in range(local):
        rank_pad[s * blocks : (s + 1) * blocks, :hands] = rank_ref[s].astype(f32)
        for b in range(blocks):
            live[s * blocks + b, :, :hands] = jnp.broadcast_to(live_ref[s, b : b + 1].astype(f32), (ACT, hands))
        all_row[me, s : s + 1] = jnp.full((1, LANES), row_ref[s], jnp.int32)
    for ref in (call_regret, fold_regret, regret_own, follow_regret, stop_regret, own_range, opp_range, values):
        ref[...] = jnp.zeros_like(ref)

    rank_columns = rank_pad[...].T

    def build(block):
        matrix_rows = rank_pad[block : block + 1, :]

        for start in range(0, wide, ROWS):
            column = rank_columns[start : start + ROWS, block : block + 1]
            difference = matrix_rows - column
            matrix[block, start : start + ROWS, :] = jnp.clip(difference, -1.0, 1.0).astype(jnp.bfloat16)

    early = min(2, local * blocks)
    for block in range(early):
        build(block)

    pl.semaphore_wait(barrier, subs - 1 + leaves - 1)

    def gather_copies(k, source, target):
        here = pl.ds(source * local, local)
        to = {"sub": target}
        return (
            pltpu.make_async_remote_copy(
                src_ref=range_ref, dst_ref=all_range.at[here], send_sem=range_send.at[k], recv_sem=range_recv.at[source],
                device_id=to, device_id_type=pl.DeviceIdType.MESH),
            pltpu.make_async_remote_copy(
                src_ref=value_ref, dst_ref=all_value.at[source], send_sem=value_send.at[k], recv_sem=value_recv.at[source],
                device_id=to, device_id_type=pl.DeviceIdType.MESH),
            pltpu.make_async_remote_copy(
                src_ref=all_row.at[source], dst_ref=all_row.at[source], send_sem=row_send.at[k], recv_sem=row_recv.at[source],
                device_id=to, device_id_type=pl.DeviceIdType.MESH),
        )

    def gather_start(k, carry):
        for copy in gather_copies(k, me, sub_peer(k)):
            copy.start()
        return carry

    lax.fori_loop(1, subs, gather_start, 0)
    all_range[pl.ds(me * local, local)] = range_ref[...]
    all_value[me] = value_ref[...]

    for block in range(early, local * blocks):
        build(block)

    def gather_wait(k, carry):
        source = sub_peer(k)
        for copy in gather_copies(k, source, source):
            copy.wait_recv()
        for copy in gather_copies(k, me, source):
            copy.wait_send()
        return carry

    lax.fori_loop(1, subs, gather_wait, 0)

    act_index = lax.broadcasted_iota(jnp.int32, (ACT, wide), 0)
    for s in range(local):
        row = row_ref[s]
        picked = all_range[row]
        own_range[s, :, :hands] = picked[0:1]
        opp_range[s, :, :hands] = picked[1:2]
        values[s, :, :hands] = all_value[row // local, pl.ds(lax.rem(row, local), 1), :]

    def sum_copies(step, s, source, target):
        to = {"leaf": target}
        return (
            pltpu.make_async_remote_copy(
                src_ref=sum_own.at[step, s, source], dst_ref=sum_own.at[step, s, source],
                send_sem=own_send.at[step, s, target], recv_sem=own_recv.at[step, s, source],
                device_id=to, device_id_type=pl.DeviceIdType.MESH),
            pltpu.make_async_remote_copy(
                src_ref=sum_follow.at[step, s, source], dst_ref=sum_follow.at[step, s, source],
                send_sem=follow_send.at[step, s, target], recv_sem=follow_recv.at[step, s, source],
                device_id=to, device_id_type=pl.DeviceIdType.MESH),
        )

    def joined_sums(step, s):
        for peer in leaf_peers:
            for copy in sum_copies(step, s, peer, peer):
                copy.wait_recv()
        value_own = sum_own[step, s, 0]
        follow_value = sum_follow[step, s, 0]
        for index in range(1, leaves):
            value_own = value_own + sum_own[step, s, index]
            follow_value = follow_value + sum_follow[step, s, index]
        root_value = jnp.sum(strategy[s] * value_own, axis=0, keepdims=True)
        return value_own, follow_value, root_value

    def update(step, s):
        value_own, follow_value, root_value = joined_sums(step, s)
        gadget_value = follow[s] * follow_value + (1.0 - follow[s]) * values[s]
        regret_own[s] = jnp.maximum(regret_own[s] + value_own - root_value, 0.0)
        follow_regret[s] = jnp.maximum(follow_regret[s] + follow_value - gadget_value, 0.0)
        stop_regret[s] = jnp.maximum(stop_regret[s] + values[s] - gadget_value, 0.0)

    def sweep(step, s):
        own = regret_own[s]
        plan = (own + smooth) / (jnp.sum(own, axis=0, keepdims=True) + ACT * smooth)
        strategy[s] = plan
        enter = follow_regret[s]
        go = (enter + smooth) / (enter + stop_regret[s] + 2 * smooth)
        follow[s] = go
        reach[...] = (own_range[s] * plan).astype(jnp.bfloat16).astype(f32)
        entering = jnp.broadcast_to(opp_range[s] * go, (ACT, wide))
        pot = pot_ref[s]
        factor = jnp.zeros((ACT, wide), f32)
        for a in range(ACT):
            factor = jnp.where(act_index == a, pot * (1.0 + bet_ref[s, a]), factor)
        factor = factor / hands
        used = count_ref[s]
        share = 1.0 / jnp.full((1, wide), used.astype(f32), f32)

        def one_block(b, carry):
            part_own, part_follow = carry
            block = s * blocks + b
            mask = live[block]
            call = call_regret[block]
            fold = fold_regret[block]
            call_prob = (call + smooth) / (call + fold + 2 * smooth)
            stay = 1.0 - call_prob
            own_live = reach[...] * mask
            reach_call = ((entering * call_prob) * mask).astype(jnp.bfloat16)
            columns = jnp.concatenate([reach_call, own_live.astype(jnp.bfloat16)], axis=0)
            applied = jnp.dot(columns, matrix[block], preferred_element_type=f32)
            fold_mass = jnp.sum(mask * (entering * stay), axis=1, keepdims=True) / hands
            own_mass = jnp.sum(own_live, axis=1, keepdims=True) / hands
            scaled = factor * mask
            weight = share * jnp.where(leaf * blocks + b < used, 1.0, 0.0)
            part_own = part_own + weight * (scaled * applied[:ACT] + mask * (pot * fold_mass))
            call_value = scaled * applied[ACT:]
            fold_value = -mask * (pot * own_mass)
            node_value = call_prob * call_value + stay * fold_value
            part_follow = part_follow + weight * jnp.sum(node_value, axis=0, keepdims=True)
            call_regret[block] = jnp.maximum(call + call_value - node_value, 0.0)
            fold_regret[block] = jnp.maximum(fold + fold_value - node_value, 0.0)
            return part_own, part_follow

        part_own, part_follow = lax.fori_loop(
            0, blocks, one_block, (jnp.zeros((ACT, wide), f32), jnp.zeros((1, wide), f32)))
        sum_own[step, s, leaf] = part_own
        sum_follow[step, s, leaf] = part_follow
        for peer in leaf_peers:
            for copy in sum_copies(step, s, leaf, peer):
                copy.start()

    def iteration(step, carry):
        for s in range(local):
            @pl.when(step > 0)
            def _():
                update(step - 1, s)

            sweep(step, s)
        return carry

    lax.fori_loop(0, ITERS, iteration, 0)

    def final_copy(s, k, source, target):
        return pltpu.make_async_remote_copy(
            src_ref=final.at[source, s], dst_ref=final.at[source, s],
            send_sem=final_send.at[s, k], recv_sem=final_recv.at[s, source],
            device_id={"sub": target}, device_id_type=pl.DeviceIdType.MESH)

    for s in range(local):
        value_own, follow_value, root_value = joined_sums(ITERS - 1, s)
        final[me, s, 0:1] = root_value
        final[me, s, 1:2] = jnp.maximum(values[s], follow_value)

        def final_start(k, carry):
            final_copy(s, k, me, sub_peer(k)).start()
            return carry

        lax.fori_loop(1, subs, final_start, 0)

    def sums_sent(step, carry):
        for s in range(local):
            for peer in leaf_peers:
                for copy in sum_copies(step, s, leaf, peer):
                    copy.wait_send()
        return carry

    lax.fori_loop(0, ITERS, sums_sent, 0)

    def final_wait(k, carry):
        source = sub_peer(k)
        for s in range(local):
            final_copy(s, k, source, source).wait_recv()
            final_copy(s, k, me, source).wait_send()
        return carry

    lax.fori_loop(1, subs, final_wait, 0)

    def pick(source, rows):
        picked = list(rows)
        for s in range(local):
            named = all_row[source, s : s + 1, 0:1]
            result = final[source, s]
            for q in range(local):
                picked[q] = jnp.where(named == me * local + q, result, picked[q])
        return tuple(picked)

    rows = lax.fori_loop(0, subs, pick, tuple(jnp.zeros((2, wide), f32) for _ in range(local)))
    for q in range(local):
        out_ref[q] = rows[q][:, :hands]


def solution(mesh):
    subs = mesh.shape["sub"]
    leaves = mesh.shape["leaf"]

    def shards(child_row, counts, live_mask, hand_rank, bet_size, pot_size, trunk_ranges, trunk_values):
        local, blocks, hands = live_mask.shape
        wide = -(-hands // LANES) * LANES
        total = local * blocks
        f32 = jnp.float32
        smem = pl.BlockSpec(memory_space=pltpu.SMEM)
        vmem = pl.BlockSpec(memory_space=pltpu.VMEM)
        dma = pltpu.SemaphoreType.DMA
        scratch = [
            pltpu.VMEM((total, wide, wide), jnp.bfloat16),
            pltpu.VMEM((total, wide), f32),
            pltpu.VMEM((total, ACT, wide), f32),
            pltpu.VMEM((total, ACT, wide), f32),
            pltpu.VMEM((total, ACT, wide), f32),
            pltpu.VMEM((local, ACT, wide), f32),
            pltpu.VMEM((local, 1, wide), f32),
            pltpu.VMEM((local, 1, wide), f32),
            pltpu.VMEM((local, 1, wide), f32),
            pltpu.VMEM((local, 1, wide), f32),
            pltpu.VMEM((local, 1, wide), f32),
            pltpu.VMEM((local, ACT, wide), f32),
            pltpu.VMEM((local, 1, wide), f32),
            pltpu.VMEM((ACT, wide), f32),
            pltpu.VMEM((ITERS, local, leaves, ACT, wide), f32),
            pltpu.VMEM((ITERS, local, leaves, 1, wide), f32),
            pltpu.VMEM((subs * local, 2, hands), f32),
            pltpu.VMEM((subs, local, hands), f32),
            pltpu.VMEM((subs, local, LANES), jnp.int32),
            pltpu.VMEM((subs, local, 2, wide), f32),
        ]
        scratch += [dma((subs,))] * 6 + [dma((ITERS, local, leaves))] * 4 + [dma((local, subs))] * 2
        return pl.pallas_call(
            functools.partial(solve_kernel, subs, leaves, hands, wide, local, blocks),
            out_shape=jax.ShapeDtypeStruct((local, 2, hands), f32),
            in_specs=[smem, smem, smem, smem, vmem, vmem, vmem, vmem],
            out_specs=vmem,
            scratch_shapes=scratch,
            compiler_params=pltpu.CompilerParams(
                collective_id=0, has_side_effects=True, vmem_limit_bytes=60 * 1024 * 1024),
            name="gadget_sweep",
        )(child_row, counts, bet_size, pot_size, live_mask, hand_rank, trunk_ranges, trunk_values)

    in_specs = (
        P("sub"),
        P("sub"),
        P("sub", "leaf", None),
        P("sub", "leaf", None),
        P("sub", None),
        P("sub"),
        P("sub", None, None),
        P("sub", None),
    )
    return jax.shard_map(shards, mesh=mesh, in_specs=in_specs, out_specs=P("sub", None, None), check_vma=False)
```

time: 373 us -> 51.8 us (0.14)
  blocking collectives: 153 us -> 0 us
  waiting for transfers between devices: 94.3 us -> 0 us
  matrix products: 77.9 us -> 0 us
  Pallas kernels: 0 us -> 50.2 us
  other arithmetic: 17.5 us -> 0 us
  between operations: 14.2 us -> 0.01 us
  local copies, waits for them, and re-layouts: 15.1 us -> 1.34 us
    psum x4 -> x0, waiting for transfers between devices: 94.2 us -> none  [shards(): value_own, follow_value = lax.psum((partial_own, partial_follow), 'leaf')]
    dot_general x64 -> x0, matrix products: 77.9 us -> none  [one_block(): lax.dot_general(column_set, matrix, (((1,), (1,)), ((), ())), preferred_e...]
    all_gather x3 -> x0, blocking collectives: 74.6 us -> none  [the longest x1 32.6 us: shards(): lax.all_gather(trunk_ranges, 'sub', axis=0, tiled=True)]
    pallas_call x0 -> x1, Pallas kernels: none -> 50.2 us  [shards(): pl.pallas_call(functools.partial(solve_kernel, subs, leaves, hands, wide,...]
    psum x4 -> x0, blocking collectives: 40.6 us -> none  [shards(): value_own, follow_value = lax.psum((partial_own, partial_follow), 'leaf')]
    unnamed x1 -> x0, blocking collectives: 37.5 us -> none
    slice x67 -> x0, local copies, waits for them, and re-layouts: 8.78 us -> none  [the longest x32 3.44 us: one_block(): rows_live = live_row[offset:offset + half_rows]]
    reduce_sum x11 -> x0, other arithmetic: 6.39 us -> none  [the longest x4 2.96 us: shards(): partial_follow = jnp.sum(weight * node_value, axis=(1, 2))]
  transfers between devices with their start and end apart: 4 -> 0, of which waited for: 3 -> 0; matrix products, arithmetic and copies ran while one was open for 1% -> 0% of each run, Pallas kernels for 0% -> 0%
where the time goes in v1:
time: 51.8 us; the launch traced here: 51.5 us
  Pallas kernels  50.2 us (97%)
  local copies, waits for them, and re-layouts  1.34 us (3%)
    pallas_call x1, Pallas kernels, shards(): pl.pallas_call(functools.partial(solve_kernel, subs, leaves, hands, wide,...  50.2 us
    unnamed x1, local copies, waits for them, and re-layouts  1.34 us

profile of v1, /device:TPU:0, one launch (start us, length us, event | category | flops | bytes accessed | tf_op | source)
XLA Modules:
  0.0 51.5 jit_solution(4078666391424166617)
XLA Ops:
  0.0 50.2 %gadget_sweep.1 = f32[2,2,1326]{2,1,0:T(2,128)} custom-call(s32[2]{0:T(128)} %row_ref.1, s32[2]{0:T(128)} %count_ref.1, f32[2,8]{1,0:T(2,128)} %bet_ref.1, f32[2]{0:T(128)} %pot_ref.1, s32[2,4,1326]{2,1,0:T(4,128)} %live_ref.1, s32[2,4,1326]{2,1,0:T(4,128)} %rank_ref.1, f32[2,2,1326]{2,1,0:T(2,128)} %range_ref.1, f32[2,1326]{1,0:T(2,128)} %value_ref.1), custom_call_target="tpu_custom_call" | custom-call | tf_op jit(solution)/shard_map/gadget_sweep/pallas_call | solution.py:293
  50.2 1.3 %copy.10 = f32[2,2,1326]{2,1,0:T(2,128)} copy(f32[2,2,1326]{2,1,0:T(2,128)} %gadget_sweep.1) | data formatting | bytes 42432
